TPU v7x, 32 devices: a whole 2x2x4 slice. The times are simulated.
32 devices in a mesh: vocab: 16 (over z, y, core), tok: 2 (over x).
Axes of the slice: x: 2, y: 2, z: 4, core: 2. Of those that a mesh axis runs over, the one named last changes fastest.
Arguments:
- hidden: bfloat16 [2048, 4096], P('tok', 'vocab'), may hold values from -64 to 64
- weight: bfloat16 [4096, 16384], P(None, 'vocab'), may hold values from -1 to 1
- proj_in: bfloat16 [4096, 64], replicated, may hold values from -0.09375 to 0.09375
- proj_out: bfloat16 [16384, 64], P('vocab'), may hold values from -6 to 6
- targets: int32 [2048], P('tok'), may hold values from 0 to 16383
- segments: int32 [2, 1024], P('tok'), may hold values from 0 to 15, never falling along the last dimension, each value on 1 to 128 neighbouring positions
- queries: bfloat16 [2048, 4096], P(('vocab', 'tok')), may hold values from -0.059814453 to 0.059814453
Outputs:
- scores: float32 [32, 2048], P(None, ('vocab', 'tok'))
Inputs may be any that keep to these rules, and one draw needn't show every extreme that they name: `segments`: each group's row numbers its documents 0 to 15 in order, each with 1 to 128 tokens.
All inputs are finite; a program needn't handle non-finite values.
Results may differ from a plain program's by a relative error of at most 0.0095.
Values may be sent and summed in bfloat16 or wider, within the bound.
A program may use at most 64 MiB of HBM per device.

v0:
```python
import jax
import jax.numpy as jnp
from jax import lax
from jax.sharding import PartitionSpec as P

DOC_V = 1


def joined(value, axis, join):
    pieces = jax.tree.map(lambda part: lax.all_gather(part, axis), value)
    head = jax.tree.map(lambda part: part[0], pieces)
    tail = jax.tree.map(lambda part: part[1:], pieces)
    subtotal, _ = lax.scan(lambda subtotal, share: (join(subtotal, share), None), head, tail)
    return subtotal


def split_parts(values):
    high = values.astype(jnp.bfloat16)
    low = (values - high.astype(jnp.float32)).astype(jnp.bfloat16)
    return (high, low)


def outer_sums(member, left_side, right_side):
    count = left_side.shape[0]
    member_half = member.astype(jnp.bfloat16)
    left_high, left_low = split_parts(left_side)
    right_high, right_low = split_parts(right_side)
    spread_high = (member_half[:, :, None] * left_high[:, None, :]).reshape(count, -1)
    spread_low = (member_half[:, :, None] * left_low[:, None, :]).reshape(count, -1)
    dims = (((0,), (0,)), ((), ()))
    result = lax.dot_general(spread_high, right_high, dims, preferred_element_type=jnp.float32)
    result = result + lax.dot_general(
        spread_high, right_low, dims, preferred_element_type=jnp.float32
    )
    result = result + lax.dot_general(
        spread_low, right_high, dims, preferred_element_type=jnp.float32
    )
    return result.reshape(member.shape[1], -1)


def join_stats(earlier, later):
    highest = jnp.maximum(earlier[0], later[0])
    summed = earlier[1] * jnp.exp(earlier[0] - highest) + later[1] * jnp.exp(later[0] - highest)
    return (highest, summed)


def per_device(hidden, weight, proj_in, proj_out, targets, segments, queries):
    vocab_local = weight.shape[1]
    columns = lax.all_gather(hidden, "vocab", axis=1, tiled=True)
    logits = jnp.dot(columns, weight, preferred_element_type=jnp.float32)
    left_side = jnp.dot(columns, proj_in, preferred_element_type=jnp.float32)
    local_top = jnp.max(logits, axis=1)
    local_total = jnp.sum(jnp.exp(logits - local_top[:, None]), axis=1)
    top, total = joined((local_top, local_total), "vocab", join_stats)
    expo = jnp.exp(logits - top[:, None])
    offset = lax.axis_index("vocab") * vocab_local
    column = jnp.arange(vocab_local, dtype=jnp.int32)
    onehot = ((targets - offset)[:, None] == column[None, :]).astype(jnp.float32)
    resid = (expo / total[:, None] - onehot).astype(jnp.bfloat16)
    partial_value = jnp.dot(resid, proj_out, preferred_element_type=jnp.float32)
    labels = segments[0]
    right_side = lax.psum(partial_value, "vocab")
    owned = lax.axis_index("vocab") * DOC_V + jnp.arange(DOC_V, dtype=jnp.int32)
    member = (labels[:, None] == owned[None, :]).astype(jnp.float32)
    grads = outer_sums(member, left_side, right_side)
    grads = grads.astype(jnp.bfloat16)
    group_grads = lax.all_gather(grads, "vocab", axis=0, tiled=True)
    return lax.dot_general(
        lax.all_gather(group_grads, "tok", axis=0, tiled=True),
        queries,
        (((1,), (1,)), ((), ())),
        preferred_element_type=jnp.float32,
    )


def solution(mesh):
    return jax.shard_map(
        per_device,
        mesh=mesh,
        in_specs=(
            P("tok", "vocab"),
            P(None, "vocab"),
            P(),
            P("vocab", None),
            P("tok"),
            P("tok", None),
            P(("vocab", "tok"), None),
        ),
        out_specs=P(None, ("vocab", "tok")),
        check_vma=False,
    )
```

profile of v0, /device:TPU:0, one launch (start us, length us, event | category | flops | bytes accessed | tf_op | source)
XLA Modules:
  0.0 273.4 jit_solution(15972344849614150023)
XLA Ops:
  6.5 0.7 all-gather.5.cloned.1.call-update
  7.3 0.0 all-reduce.2.cloned.1.call-start
  7.3 0.7 fusion.14
  8.0 0.7 broadcast_subtract_fusion
  8.7 81.2 %all-gather.5.cloned.1.call-done = bf16[1024,4096]{1,0:T(8,128)(2,1)} async-done(((bf16[1024,256]{1,0:T(8,128)(2,1)}), bf16[1024,4096]{1,0:T(8,128)(2,1)}) %all-gather.5.cloned.1.call-update) | async-done | bytes 8388624 | tf_op jit(solution)/shard_map/all_gather | solution.py:49
  90.0 13.5 %fusion.18 = (f32[1024]{0:T(1024)S(1)}, f32[1024,1024]{0,1:T(8,128)S(1)}) fusion(bf16[1024,4096]{1,0:T(8,128)(2,1)} %all-gather.5.cloned.1.call-done, bf16[4096,1024]{1,0:T(8,128)(2,1)} %param.10), kind=kOutput, calls=%fused_computation.30 | convolution fusion | flops 8590982144 | bytes 20975616 | tf_op jit(solution)/shard_map/dot_general | solution.py:50
  103.4 0.0 copy-start.3
  103.5 18.8 %all-gather = f32[16384]{0:T(1024)S(1)} all-gather(f32[1024]{0:T(1024)S(1)} %get-tuple-element.49), channel_id=2, replica_groups=mesh['vocab'=16,'tok'=2] {'vocab'}, dimensions={0}, use_global_device_ids=true | all-gather | bytes 69632 | tf_op jit(solution)/shard_map/all_gather | solution.py:10
  122.3 0.6 exponential_reduce_fusion
  122.9 17.8 %all-gather.1 = f32[16384]{0:T(1024)S(1)} all-gather(f32[1024]{0:T(1024)S(1)} %exponential_reduce_fusion), channel_id=3, replica_groups=mesh['vocab'=16,'tok'=2] {'vocab'}, dimensions={0}, use_global_device_ids=true | all-gather | bytes 69632 | tf_op jit(solution)/shard_map/all_gather | solution.py:10
  140.8 0.8 while.12
  141.6 4.2 %fusion = f32[1024,64]{0,1:T(8,128)} fusion(bf16[1024,64]{0,1:T(8,128)(2,1)S(1)} %copy-done.3, f32[1024,1024]{0,1:T(8,128)} %copy-done.1, s32[1024]{0:T(1024)S(1)} %broadcast_subtract_fusion, f32[1024]{0:T(1024)S(1)} %get-tuple-element.34, f32[1024]{0:T(1024)S(1)} %get-tuple-element.33), kind=kOutput, calls=%fused_computation.6 | convolution fusion | flops 140509184 | bytes 4599808 | tf_op jit(solution)/shard_map/dot_general | solution.py:60
  145.8 0.0 all-reduce.2.cloned.1.call-update
  145.9 0.0 copy-start.2
  145.9 6.1 %fusion.19 = f32[1024,64]{0,1:T(8,128)S(1)} fusion(bf16[1024,4096]{1,0:T(8,128)(2,1)} %all-gather.5.cloned.1.call-done, bf16[4096,64]{0,1:T(8,128)(2,1)S(1)} %copy-done), kind=kOutput, calls=%fused_computation.31 | convolution fusion | flops 536870912 | bytes 9175040 | tf_op jit(solution)/shard_map/dot_general | solution.py:51
  152.0 82.0 %all-reduce.2.cloned.1.call-done = f32[1024,64]{0,1:T(8,128)} async-done(((f32[1024,64]{0,1:T(8,128)}), f32[1024,64]{0,1:T(8,128)}) %all-reduce.2.cloned.1.call-update) | async-done | bytes 262160 | tf_op jit(solution)/shard_map/psum | solution.py:62
  234.0 1.1 fusion.5
  235.1 1.2 convolution_add_fusion.1
  236.3 1.1 fusion.1
  237.5 0.1 reshape.53
  237.6 21.5 %all-gather.2 = bf16[16,1,4096]{2,1,0:T(2,128)(2,1)S(1)} all-gather(bf16[1,1,4096]{2,1,0:T(2,128)(2,1)S(1)} %reshape.53), channel_id=1, replica_groups=mesh['vocab'=16,'tok'=2] {'vocab'}, dimensions={0}, use_global_device_ids=true | all-gather | bytes 139264 | tf_op jit(solution)/shard_map/all_gather | solution.py:67
  259.1 0.1 copy.11
  259.3 6.4 %all_gather.27 = bf16[32,4096]{1,0:T(8,128)(2,1)S(1)} all-gather(bf16[16,4096]{1,0:T(8,128)(2,1)S(1)} %bitcast.16), channel_id=1, replica_groups=mesh['vocab'=16,'tok'=2] {'tok'}, dimensions={0}, use_global_device_ids=true | all-gather | bytes 393216 | tf_op jit(solution)/shard_map/all_gather | solution.py:69
  265.7 0.9 fusion.20
  (43 shorter events, 0.4 us)
Async XLA Ops:
  6.5 139.3 %copy-start = (bf16[4096,64]{0,1:T(8,128)(2,1)S(1)}, bf16[4096,64]{0,1:T(8,128)(2,1)}, u32[]{:S(2)}) copy-start(bf16[4096,64]{0,1:T(8,128)(2,1)} %param.11) | copy-start | bytes 1572868
  6.5 83.4 %all-gather.5.cloned.1.call-start = ((), (), s32[]{:S(2)}) async-start(), calls=%async_computation | async-start | bytes 8912896 | tf_op jit(solution)/shard_map/all_gather | solution.py:49
  7.3 226.7 %all-reduce.2.cloned.1.call-start = ((), (), s32[]{:S(2)}) async-start(), calls=%async_computation.1 | async-start | bytes 524288 | tf_op jit(solution)/shard_map/psum | solution.py:62
  103.4 18.9 %copy-start.1 = (f32[1024,1024]{0,1:T(8,128)}, f32[1024,1024]{0,1:T(8,128)S(1)}, u32[]{:S(2)}) copy-start(f32[1024,1024]{0,1:T(8,128)S(1)} %get-tuple-element.50) | copy-start | bytes 12582916
  103.4 38.2 %copy-start.3 = (bf16[1024,64]{0,1:T(8,128)(2,1)S(1)}, bf16[1024,64]{0,1:T(8,128)(2,1)}, u32[]{:S(2)}) copy-start(bf16[1024,64]{0,1:T(8,128)(2,1)} %param.12) | copy-start | bytes 393220
  145.9 119.8 %copy-start.2 = (bf16[64,4096]{1,0:T(8,128)(2,1)S(1)}, bf16[64,4096]{1,0:T(8,128)(2,1)}, u32[]{:S(2)}) copy-start(bf16[64,4096]{1,0:T(8,128)(2,1)} %param.15) | copy-start | bytes 1572868
Sparse Core Ops, SparseCore 0:
  9.5 80.4 all-gather.4
  146.0 87.9 all-reduce.1
where the time goes:
time: 274 us; the launch traced here: 273 us
  waiting for transfers between devices  164 us (60%)
  blocking collectives  64.6 us (24%)
  matrix products  28.1 us (10%)
  between operations  13.5 us (5%)
    psum x1, waiting for transfers between devices, per_device(): right_side = lax.psum(partial_value, 'vocab')  82 us
    all_gather x1, waiting for transfers between devices, per_device(): columns = lax.all_gather(hidden, 'vocab', axis=1, tiled=True)  81.2 us
    all_gather x2, blocking collectives, joined(): pieces = jax.tree.map(lambda part: lax.all_gather(part, axis), value)  36.7 us
    all_gather x1, blocking collectives, per_device(): group_grads = lax.all_gather(grads, 'vocab', axis=0, tiled=True)  21.5 us
    dot_general x1, matrix products, per_device(): logits = jnp.dot(columns, weight, preferred_element_type=jnp.float32)  13.5 us
    all_gather x1, blocking collectives, per_device(): lax.all_gather(group_grads, 'tok', axis=0, tiled=True)  6.41 us
    dot_general x1, matrix products, per_device(): left_side = jnp.dot(columns, proj_in, preferred_element_type=jnp.float32)  6.09 us
  transfers between devices with their start and end apart: 2, of which 2 were waited for; matrix products, arithmetic and copies ran while one was open for 3% of the time, Pallas kernels for 0%

commit v1 on v0

v1 whole, which is shorter than its diff:
```python
import functools

import jax
import jax.numpy as jnp
from jax import lax
from jax.experimental import pallas as pl
from jax.experimental.pallas import tpu as pltpu
from jax.sharding import PartitionSpec as P

DOC_V = 1
MESH = pl.DeviceIdType.MESH
LANES = 128


def chip_of(place, chips):
    back = place // (chips // 2)
    return (1 - back) * 2 * place + back * (2 * (chips - 1 - place) + 1)


def place_of(chip, chips):
    odd, half = chip % 2, chip // 2
    return odd * (chips - 1 - half) + (1 - odd) * half


def kernel(
    devices,
    h_ref, w_hbm, pin_ref, pa_ref, pb_ref, tgt_ref, seg_ref,
    out_ref,
    held, w_ref, logits, left, spread, msg, stat, got_msg, got_stat, weights, right,
    w_sem, ring_send, ring_recv, mate_send, mate_recv, own_send, own_recv,
    msg_send, msg_recv, stat_send, stat_recv, right_send, right_recv,
):
    chips, steps = devices // 2, devices // 4
    tokens, depth = h_ref.shape
    vocab = w_ref.shape[1]
    rank = pin_ref.shape[1]
    half_rows = tokens // 2
    block = tokens // devices
    docs = out_ref.shape[0] // rank
    me = lax.axis_index("vocab")
    core = me % 2
    place = place_of(me // 2, chips)
    mate = me + 1 - 2 * core
    nexts = [
        2 * chip_of((place + 1) % chips, chips) + core,
        2 * chip_of((place + chips - 1) % chips, chips) + core,
    ]

    barrier = pltpu.get_barrier_semaphore()
    for k in range(1, devices):
        pl.semaphore_signal(
            barrier, inc=1, device_id={"vocab": (me + k) % devices}, device_id_type=MESH
        )
    w_copy = pltpu.make_async_copy(w_hbm, w_ref, w_sem)
    w_copy.start()
    pl.semaphore_wait(barrier, devices - 1)

    sent = []

    def remote(src, dst, send_sem, recv_sem, device):
        return pltpu.make_async_remote_copy(
            src_ref=src, dst_ref=dst, send_sem=send_sem, recv_sem=recv_sem,
            device_id={"vocab": device}, device_id_type=MESH,
        )

    def start(*args):
        copy = remote(*args)
        copy.start()
        sent.append(copy)

    def source_of(way, step):
        shift = (chips - step) if way == 0 else step
        return 2 * chip_of((place + shift) % chips, chips) + core

    def piece(slot, half):
        return held.at[slot, pl.ds(half * half_rows, half_rows), :]

    def own_piece(half):
        return h_ref.at[pl.ds(half * half_rows, half_rows), :]

    def travels(way, step, half):
        return step < steps - 1 or (step == steps - 1 and half == way)

    for half in range(2):
        for way in range(2):
            if travels(way, 0, half):
                start(
                    own_piece(half), piece(me, half),
                    ring_send.at[way, 0, half], ring_recv.at[way, 0, half], nexts[way],
                )
    for half in range(2):
        start(own_piece(half), piece(me, half), own_send.at[half], own_recv.at[half], mate)

    tile = 256 if tokens % 256 == 0 else tokens

    def consume(load, slot, first=False):
        deep = pl.ds(pl.multiple_of(slot * depth, depth), depth)

        def body(i, carry):
            rows = pl.ds(pl.multiple_of(i * tile, tile), tile)
            states = load(rows)
            value = jnp.dot(states, w_ref[deep, :], preferred_element_type=jnp.float32)
            side = jnp.dot(states, pin_ref[deep, :], preferred_element_type=jnp.float32)
            if first:
                logits[rows, :] = value
                left[rows, 0:rank] = side
            else:
                logits[rows, :] += value
                left[rows, 0:rank] += side
            return carry

        lax.fori_loop(0, tokens // tile, body, 0)

    left[...] = jnp.zeros_like(left)
    w_copy.wait()
    consume(lambda rows: h_ref[rows, :], me, first=True)
    for half in range(2):
        remote(
            own_piece(half), piece(mate, half), own_send.at[half], own_recv.at[half], mate
        ).wait_recv()
    consume(lambda rows: held[mate, rows, :], mate)

    for step in range(steps):
        for half in range(2):
            for way in range(2):
                if not travels(way, step, half):
                    continue
                slot = source_of(way, step + 1)
                here = piece(slot, half)
                remote(
                    here, here, ring_send.at[way, step, half],
                    ring_recv.at[way, step, half], nexts[way],
                ).wait_recv()
                if travels(way, step + 1, half):
                    start(
                        here, here, ring_send.at[way, step + 1, half],
                        ring_recv.at[way, step + 1, half], nexts[way],
                    )
                start(
                    here, here, mate_send.at[way, step, half],
                    mate_recv.at[way, step, half], mate,
                )
        slots = [source_of(way, step + 1) for way in range(2 if step < steps - 1 else 1)]
        for slot in slots:
            consume(lambda rows, slot=slot: held[slot, rows, :], slot)
        flip = 1 - 2 * core
        for half in range(2):
            for way in range(2):
                if travels(way, step, half):
                    there = piece(source_of(way, step + 1) + flip, half)
                    remote(
                        there, there, mate_send.at[way, step, half],
                        mate_recv.at[way, step, half], mate,
                    ).wait_recv()
        for slot in slots:
            consume(lambda rows, slot=slot: held[slot + flip, rows, :], slot + flip)

    lane = lax.broadcasted_iota(jnp.int32, (LANES, LANES), 1)
    column = lax.broadcasted_iota(jnp.int32, (LANES, vocab), 1)
    offset = me * vocab

    def soften(i, carry):
        rows = pl.ds(pl.multiple_of(i * LANES, LANES), LANES)
        value = logits[rows, :]
        top = jnp.max(value, axis=1, keepdims=True)
        expo = jnp.exp(value - top)
        hit = column == tgt_ref[rows, :] - offset
        rest = jnp.where(hit, 0.0, expo)
        total = jnp.sum(expo, axis=1, keepdims=True)
        others = jnp.sum(rest, axis=1, keepdims=True)
        onehot = jnp.where(hit, 1.0, 0.0).astype(jnp.bfloat16)
        both = jnp.dot(rest.astype(jnp.bfloat16), pa_ref[...], preferred_element_type=jnp.float32)
        both += jnp.dot(onehot, pb_ref[...], preferred_element_type=jnp.float32)
        msg[rows, :] = both.astype(jnp.bfloat16)
        packed = jnp.where(
            lane == 0, top, jnp.where(lane == 1, total, jnp.where(lane == 2, others, 0.0))
        )
        stat[i] = jnp.transpose(packed)[0:8, :]
        return carry

    lax.fori_loop(0, tokens // LANES, soften, 0)

    per_tile = LANES // block

    def rows_of(device):
        return pl.ds(pl.multiple_of(device * block, block), block)

    for k in range(1, devices):
        peer = (me + k) % devices
        start(
            stat.at[peer // per_tile], got_stat.at[me],
            stat_send.at[k - 1], stat_recv.at[k - 1], peer,
        )
        start(
            msg.at[rows_of(peer), :], got_msg.at[me],
            msg_send.at[k - 1], msg_recv.at[k - 1], peer,
        )
    got_stat[me] = stat[me // per_tile]
    got_msg[me] = msg[rows_of(me), :]

    turned = jnp.transpose(left[...])[0:rank, :]
    labels = seg_ref[...]

    def mark(d, carry):
        rows = pl.ds(pl.multiple_of(d * rank, rank), rank)
        spread[rows, :] = jnp.where(labels == d, turned, 0.0).astype(jnp.bfloat16)
        return carry

    lax.fori_loop(0, docs, mark, 0)

    for k in range(1, devices):
        peer = (me + devices - k) % devices
        remote(
            got_stat.at[peer], got_stat.at[peer],
            stat_send.at[k - 1], stat_recv.at[k - 1], peer,
        ).wait_recv()
    tops = [got_stat[d, 0:1, :] for d in range(devices)]
    top = functools.reduce(jnp.maximum, tops)
    scale = [jnp.exp(each - top) for each in tops]
    total = sum(scale[d] * got_stat[d, 1:2, :] for d in range(devices))
    others = sum(scale[d] * got_stat[d, 2:3, :] for d in range(devices))
    weights[...] = jnp.zeros_like(weights)
    for d in range(devices):
        weights[d : d + 1, :] = scale[d] / total
    weights[devices : devices + 1, :] = others / total
    weights[...] = jnp.transpose(weights[...])
    part = weights[pl.ds(pl.multiple_of((me % per_tile) * block, block), block), :]

    for k in range(1, devices):
        peer = (me + devices - k) % devices
        remote(
            got_msg.at[peer], got_msg.at[peer],
            msg_send.at[k - 1], msg_recv.at[k - 1], peer,
        ).wait_recv()
    summed = jnp.zeros((block, LANES), jnp.float32)
    plain = jnp.zeros((block, LANES), jnp.float32)
    for d in range(devices):
        value = got_msg[d].astype(jnp.float32)
        summed += value * part[:, d : d + 1]
        plain += value
    wanted = pltpu.roll(plain, rank, 1)
    inside = lax.broadcasted_iota(jnp.int32, (block, LANES), 1) < rank
    result = jnp.where(inside, summed - part[:, devices : devices + 1] * wanted, 0.0)
    right[rows_of(me), :] = result.astype(jnp.bfloat16)
    for k in range(1, devices):
        start(
            right.at[rows_of(me), :], right.at[rows_of(me), :],
            right_send.at[k - 1], right_recv.at[k - 1], (me + k) % devices,
        )
    for k in range(1, devices):
        peer = (me + devices - k) % devices
        remote(
            right.at[rows_of(peer), :], right.at[rows_of(peer), :],
            right_send.at[k - 1], right_recv.at[k - 1], peer,
        ).wait_recv()

    height = min(256, docs * rank)

    def join(i, carry):
        rows = pl.ds(pl.multiple_of(i * height, height), height)
        value = jnp.dot(spread[rows, :], right[...], preferred_element_type=jnp.float32)
        out_ref[rows, :] = value[:, 0:rank].astype(jnp.bfloat16)
        return carry

    lax.fori_loop(0, docs * rank // height, join, 0)
    for copy in sent:
        copy.wait_send()


def document_grads(devices, hidden, weight, proj_in, proj_out, targets, segments):
    tokens, depth = hidden.shape
    width, vocab = weight.shape
    rank = proj_in.shape[1]
    docs = DOC_V * devices
    steps = devices // 4
    block = tokens // devices
    gap = LANES - rank
    vmem = pl.BlockSpec(memory_space=pltpu.VMEM)
    dma = pltpu.SemaphoreType.DMA
    ring = dma((2, steps, 2))
    peers = dma((devices - 1,))
    return pl.pallas_call(
        functools.partial(kernel, devices),
        out_shape=jax.ShapeDtypeStruct((docs * rank, rank), jnp.bfloat16),
        in_specs=[vmem, pl.BlockSpec(memory_space=pl.ANY)] + [vmem] * 5,
        out_specs=vmem,
        scratch_shapes=[
            pltpu.VMEM((devices, tokens, depth), jnp.bfloat16),
            pltpu.VMEM((width, vocab), jnp.bfloat16),
            pltpu.VMEM((tokens, vocab), jnp.float32),
            pltpu.VMEM((tokens, LANES), jnp.float32),
            pltpu.VMEM((docs * rank, tokens), jnp.bfloat16),
            pltpu.VMEM((tokens, LANES), jnp.bfloat16),
            pltpu.VMEM((tokens // LANES, 8, LANES), jnp.float32),
            pltpu.VMEM((devices, block, LANES), jnp.bfloat16),
            pltpu.VMEM((devices, 8, LANES), jnp.float32),
            pltpu.VMEM((LANES, LANES), jnp.float32),
            pltpu.VMEM((tokens, LANES), jnp.bfloat16),
            dma(()), ring, ring, ring, ring, dma((2,)), dma((2,)),
            peers, peers, peers, peers, peers, peers,
        ],
        compiler_params=pltpu.CompilerParams(
            collective_id=0, has_side_effects=True, vmem_limit_bytes=60 * 1024 * 1024
        ),
    )(
        hidden, weight, proj_in,
        jnp.pad(proj_out, ((0, 0), (0, gap))), jnp.pad(proj_out, ((0, 0), (gap, 0))),
        targets[:, None], segments,
    )


def solution(mesh):
    devices = mesh.shape["vocab"]

    def per_device(hidden, weight, proj_in, proj_out, targets, segments, queries):
        grads = document_grads(
            devices, hidden, weight, proj_in, proj_out, targets, segments
        ).reshape(DOC_V * devices, -1)
        return lax.dot_general(
            lax.all_gather(grads, "tok", axis=0, tiled=True),
            queries,
            (((1,), (1,)), ((), ())),
            preferred_element_type=jnp.float32,
        )

    return jax.shard_map(
        per_device,
        mesh=mesh,
        in_specs=(
            P("tok", "vocab"),
            P(None, "vocab"),
            P(),
            P("vocab", None),
            P("tok"),
            P("tok", None),
            P(("vocab", "tok"), None),
        ),
        out_specs=P(None, ("vocab", "tok")),
        check_vma=False,
    )
```

time: 274 us -> 89.2 us (0.33)
  waiting for transfers between devices: 164 us -> 0 us
  Pallas kernels: 0 us -> 74.3 us
  blocking collectives: 64.6 us -> 6.24 us
  matrix products: 28.1 us -> 0.89 us
  between operations: 13.5 us -> 0.02 us
  local copies, waits for them, and re-layouts: 0.51 us -> 7.39 us
    psum x1 -> x0, waiting for transfers between devices: 82 us -> none  [per_device(): right_side = lax.psum(partial_value, 'vocab')]
    all_gather x1 -> x0, waiting for transfers between devices: 81.2 us -> none  [per_device(): columns = lax.all_gather(hidden, 'vocab', axis=1, tiled=True)]
    pallas_call x0 -> x1, Pallas kernels: none -> 74.3 us  [document_grads(): pl.pallas_call(functools.partial(kernel, devices), out_shape=jax.ShapeDty...]
    all_gather x4 -> x1, blocking collectives: 64.6 us -> 6.24 us  [per_device(): lax.all_gather(grads, 'tok', axis=0, tiled=True)]
    dot_general x7 -> x1, matrix products: 28.1 us -> 0.89 us  [per_device(): lax.dot_general(lax.all_gather(grads, 'tok', axis=0, tiled=True), queries...]
    unnamed x10 -> x4, local copies, waits for them, and re-layouts: 0.26 us -> 3.49 us
  transfers between devices with their start and end apart: 2 -> 0, of which waited for: 2 -> 0; matrix products, arithmetic and copies ran while one was open for 3% -> 0% of each run, Pallas kernels for 0% -> 0%
where the time goes in v1:
time: 89.2 us; the launch traced here: 88.9 us
  Pallas kernels  74.3 us (83%)
  local copies, waits for them, and re-layouts  7.39 us (8%)
  blocking collectives  6.24 us (7%)
    pallas_call x1, Pallas kernels, document_grads(): pl.pallas_call(functools.partial(kernel, devices), out_shape=jax.ShapeDty...  74.3 us
    all_gather x1, blocking collectives, per_device(): lax.all_gather(grads, 'tok', axis=0, tiled=True)  6.24 us
    unnamed x4, local copies, waits for them, and re-layouts  3.49 us

profile of v1, /device:TPU:0, one launch (start us, length us, event | category | flops | bytes accessed | tf_op | source)
XLA Modules:
  0.0 88.9 jit_solution(13268377395428697198)
XLA Ops:
  0.0 0.0 copy-start
  0.0 1.1 %copy.11 = bf16[1024,64]{1,0:T(8,128)(2,1)S(1)} copy(bf16[1024,64]{0,1:T(8,128)(2,1)} %param.10) | data formatting | bytes 262144 | tf_op args[3]
  1.1 0.9 %fusion = (bf16[1024,128]{1,0:T(8,128)(2,1)}, bf16[1024,128]{1,0:T(8,128)(2,1)}) fusion(bf16[1024,64]{1,0:T(8,128)(2,1)S(1)} %copy.11), kind=kLoop, calls=%fused_computation | loop fusion | bytes 655360 | tf_op jit(solution)/shard_map/jit(_pad)/pad | solution.py:307
  2.1 1.7 %copy.14.tgt_ref = s32[1024,1]{1,0:T(8,128)} copy(s32[1024,1]{0,1:T(1,128)} %bitcast.3) | data formatting | bytes 8192 | tf_op jit(solution)/shard_map/broadcast_in_dim | solution.py:308
  3.8 2.4 %copy.13.pin_ref = bf16[4096,64]{1,0:T(8,128)(2,1)} copy(bf16[4096,64]{0,1:T(8,128)(2,1)} %param.9) | data formatting | bytes 1048576 | tf_op args[2]
  6.2 74.3 %shard_map.73 = bf16[1024,64]{1,0:T(8,128)(2,1)} custom-call(bf16[1024,256]{1,0:T(8,128)(2,1)} %h_ref.1, bf16[4096,1024]{1,0:T(8,128)(2,1)} %w_hbm.1, bf16[4096,64]{1,0:T(8,128)(2,1)} %copy.13.pin_ref, bf16[1024,128]{1,0:T(8,128)(2,1)} %get-tuple-element.6.pa_ref, bf16[1024,128]{1,0:T(8,128)(2,1)} %get-tuple-element.5.pb_ref, s32[1024,1]{1,0:T(8,128)} %copy.14.tgt_ref, ...), custom_call_target="tpu_custom_call" | custom-call | tf_op jit(solution)/shard_map/pallas_call | solution.py:282
  80.5 1.2 %reshape.3 = bf16[16,4096]{1,0:T(8,128)(2,1)S(1)} reshape(bf16[1024,64]{1,0:T(8,128)(2,1)} %shard_map.73) | data formatting | bytes 262144 | tf_op jit(solution)/shard_map/reshape | solution.py:318
  81.7 6.2 %all_gather.3 = bf16[32,4096]{1,0:T(8,128)(2,1)S(1)} all-gather(bf16[16,4096]{1,0:T(8,128)(2,1)S(1)} %reshape.3), channel_id=1, replica_groups=mesh['vocab'=16,'tok'=2] {'tok'}, dimensions={0}, use_global_device_ids=true | all-gather | bytes 393216 | tf_op jit(solution)/shard_map/all_gather | solution.py:320
  88.0 0.0 copy-done
  88.0 0.9 %fusion.1 = f32[32,64]{1,0:T(8,128)} fusion(bf16[32,4096]{1,0:T(8,128)(2,1)S(1)} %all_gather.3, bf16[64,4096]{1,0:T(8,128)(2,1)S(1)} %copy-done), kind=kOutput, calls=%fused_computation.1 | convolution fusion | flops 16777216 | bytes 794624 | tf_op jit(solution)/shard_map/dot_general | solution.py:319
Async XLA Ops:
  0.0 88.0 %copy-start = (bf16[64,4096]{1,0:T(8,128)(2,1)S(1)}, bf16[64,4096]{1,0:T(8,128)(2,1)}, u32[]{:S(2)}) copy-start(bf16[64,4096]{1,0:T(8,128)(2,1)} %param.13) | copy-start | bytes 1572868

commit v2 on v1

v2 whole, which is shorter than its diff:
```python
import functools

import jax
import jax.numpy as jnp
from jax import lax
from jax.experimental import pallas as pl
from jax.experimental.pallas import tpu as pltpu
from jax.sharding import PartitionSpec as P

DOC_V = 1
MESH = pl.DeviceIdType.MESH
LANES = 128
ACROSS = (((1,), (1,)), ((), ()))


def chip_of(place, chips):
    back = place // (chips // 2)
    return (1 - back) * 2 * place + back * (2 * (chips - 1 - place) + 1)


def place_of(chip, chips):
    odd, half = chip % 2, chip // 2
    return odd * (chips - 1 - half) + (1 - odd) * half


def kernel(
    devices,
    groups,
    h_ref, w_hbm, pin_ref, po_ref, tgt_ref, seg_ref,
    out_ref,
    held, w_ref, logits, left, pa_ref, pb_ref, turned, spread, msg, stat, got_msg, got_stat,
    weights, right,
    w_sem, ring_send, ring_recv, mate_send, mate_recv, own_send, own_recv,
    msg_send, msg_recv, stat_send, stat_recv, right_send, right_recv,
    group_send, group_recv,
):
    chips, steps = devices // 2, devices // 4
    tokens, depth = h_ref.shape
    vocab = w_ref.shape[1]
    rank = pin_ref.shape[0]
    half_rows = tokens // 2
    block = half_rows // devices
    docs = out_ref.shape[0] // groups
    group = lax.axis_index("tok")
    me = lax.axis_index("vocab")
    core = me % 2
    place = place_of(me // 2, chips)
    mate = me + 1 - 2 * core
    nexts = [
        2 * chip_of((place + 1) % chips, chips) + core,
        2 * chip_of((place + chips - 1) % chips, chips) + core,
    ]

    barrier = pltpu.get_barrier_semaphore()
    for k in range(1, devices):
        pl.semaphore_signal(
            barrier, inc=1, device_id={"vocab": (me + k) % devices}, device_id_type=MESH
        )
    for k in range(1, groups):
        pl.semaphore_signal(
            barrier, inc=1, device_id={"tok": (group + k) % groups}, device_id_type=MESH
        )
    w_copy = pltpu.make_async_copy(w_hbm, w_ref, w_sem)
    w_copy.start()
    pl.semaphore_wait(barrier, devices + groups - 2)

    sent = []

    def remote(src, dst, send_sem, recv_sem, device, other=None):
        target = {"vocab": device} if other is None else {"tok": other}
        return pltpu.make_async_remote_copy(
            src_ref=src, dst_ref=dst, send_sem=send_sem, recv_sem=recv_sem,
            device_id=target, device_id_type=MESH,
        )

    def start(*args):
        copy = remote(*args)
        copy.start()
        sent.append(copy)

    def source_of(way, step):
        shift = (chips - step) if way == 0 else step
        return 2 * chip_of((place + shift) % chips, chips) + core

    def piece(slot, half):
        return held.at[slot, pl.ds(half * half_rows, half_rows), :]

    def own_piece(half):
        return h_ref.at[pl.ds(half * half_rows, half_rows), :]

    def travels(way, step, half):
        return step < steps - 1 or (step == steps - 1 and half == way)

    for half in range(2):
        for way in range(2):
            if travels(way, 0, half):
                start(
                    own_piece(half), piece(me, half),
                    ring_send.at[way, 0, half], ring_recv.at[way, 0, half], nexts[way],
                )
    for half in range(2):
        start(own_piece(half), piece(me, half), own_send.at[half], own_recv.at[half], mate)

    tile = 256 if tokens % 256 == 0 else tokens

    def consume(load, slot, first=False):
        deep = pl.ds(pl.multiple_of(slot * depth, depth), depth)

        def body(i, carry):
            rows = pl.ds(pl.multiple_of(i * tile, tile), tile)
            states = load(rows)
            value = jnp.dot(states, w_ref[deep, :], preferred_element_type=jnp.float32)
            side = lax.dot_general(
                states, pin_ref[:, deep], ACROSS, preferred_element_type=jnp.float32
            )
            if first:
                logits[rows, :] = value
                left[rows, 0:rank] = side
            else:
                logits[rows, :] += value
                left[rows, 0:rank] += side
            return carry

        lax.fori_loop(0, tokens // tile, body, 0)

    left[...] = jnp.zeros_like(left)
    pa_ref[...] = jnp.zeros_like(pa_ref)
    pb_ref[...] = jnp.zeros_like(pb_ref)
    pa_ref[0:rank, :] = po_ref[...]
    pb_ref[rank : 2 * rank, :] = po_ref[...]
    w_copy.wait()
    consume(lambda rows: h_ref[rows, :], me, first=True)
    for half in range(2):
        remote(
            own_piece(half), piece(mate, half), own_send.at[half], own_recv.at[half], mate
        ).wait_recv()
    consume(lambda rows: held[mate, rows, :], mate)

    flip = 1 - 2 * core

    def consume_mates(step):
        for half in range(2):
            for way in range(2):
                if travels(way, step, half):
                    there = piece(source_of(way, step + 1) + flip, half)
                    remote(
                        there, there, mate_send.at[way, step, half],
                        mate_recv.at[way, step, half], mate,
                    ).wait_recv()
        for slot in slots_of(step):
            consume(lambda rows, slot=slot: held[slot + flip, rows, :], slot + flip)

    def slots_of(step):
        return [source_of(way, step + 1) for way in range(2 if step < steps - 1 else 1)]

    for step in range(steps):
        for half in range(2):
            for way in range(2):
                if not travels(way, step, half):
                    continue
                slot = source_of(way, step + 1)
                here = piece(slot, half)
                remote(
                    here, here, ring_send.at[way, step, half],
                    ring_recv.at[way, step, half], nexts[way],
                ).wait_recv()
                if travels(way, step + 1, half):
                    start(
                        here, here, ring_send.at[way, step + 1, half],
                        ring_recv.at[way, step + 1, half], nexts[way],
                    )
                start(
                    here, here, mate_send.at[way, step, half],
                    mate_recv.at[way, step, half], mate,
                )
            if half == 0 and step > 0:
                consume_mates(step - 1)
        for slot in slots_of(step):
            consume(lambda rows, slot=slot: held[slot, rows, :], slot)
    consume_mates(steps - 1)

    lane = lax.broadcasted_iota(jnp.int32, (LANES, LANES), 1)
    column = lax.broadcasted_iota(jnp.int32, (LANES, vocab), 1)
    offset = me * vocab

    tiles = half_rows // LANES
    per_tile = LANES // block

    def soften(part, i):
        rows = pl.ds(pl.multiple_of(part * half_rows + i * LANES, LANES), LANES)
        value = logits[rows, :]
        top = jnp.max(value, axis=1, keepdims=True)
        expo = jnp.exp(value - top)
        wanted = jnp.broadcast_to(
            tgt_ref[:, rows].astype(jnp.float32), (LANES, LANES)
        )
        wanted = jnp.transpose(wanted)[:, 0:1].astype(jnp.int32)
        hit = column == wanted - offset
        rest = jnp.where(hit, 0.0, expo)
        total = jnp.sum(expo, axis=1, keepdims=True)
        others = jnp.sum(rest, axis=1, keepdims=True)
        onehot = jnp.where(hit, 1.0, 0.0).astype(jnp.bfloat16)
        both = lax.dot_general(
            rest.astype(jnp.bfloat16), pa_ref[...], ACROSS, preferred_element_type=jnp.float32
        )
        both += lax.dot_general(
            onehot, pb_ref[...], ACROSS, preferred_element_type=jnp.float32
        )
        spot = pl.ds(pl.multiple_of(i * LANES, LANES), LANES)
        msg[part, spot, :] = both.astype(jnp.bfloat16)
        return [top, total, others]

    def rows_of(device):
        return pl.ds(pl.multiple_of(device * block, block), block)

    def push(i):
        for d in range(per_tile):
            peer = i * per_tile + d
            away = (peer + devices - me) % devices

            @pl.when(peer != me)
            def _():
                remote(
                    stat.at[i], got_stat.at[me], stat_send.at[away], stat_recv.at[away], peer
                ).start()
                remote(
                    msg.at[:, rows_of(peer), :], got_msg.at[me],
                    msg_send.at[away], msg_recv.at[away], peer,
                ).start()

    first = me // per_tile + 1

    def stage(n, carry):
        i = (first + n) % tiles
        values = soften(0, i) + soften(1, i)
        packed = jnp.zeros((LANES, LANES), jnp.float32)
        for at, each in enumerate(values):
            packed = jnp.where(lane == at, each, packed)
        stat[i] = jnp.transpose(packed)[0:8, :]

        @pl.when(n > 0)
        def _():
            push((first + n + tiles - 1) % tiles)

        return carry

    lax.fori_loop(0, tiles, stage, 0)
    push((first + tiles - 1) % tiles)
    got_stat[me] = stat[me // per_tile]
    got_msg[me] = msg[:, rows_of(me), :]

    turned[...] = jnp.transpose(left[...])
    labels = seg_ref[...]
    member = labels == lax.broadcasted_iota(jnp.int32, (docs, tokens), 0)

    def mark(a, carry):
        rows = pl.ds(pl.multiple_of(a * docs, docs), docs)
        spread[rows, :] = jnp.where(member, turned[pl.ds(a, 1), :], 0.0).astype(jnp.bfloat16)
        return carry

    lax.fori_loop(0, rank, mark, 0)

    for k in range(1, devices):
        peer = (me + devices - k) % devices
        remote(
            got_stat.at[peer], got_stat.at[peer], stat_send.at[k], stat_recv.at[k], peer
        ).wait_recv()
    parts = []
    for p in range(2):
        tops = [got_stat[d, 3 * p : 3 * p + 1, :] for d in range(devices)]
        top = functools.reduce(jnp.maximum, tops)
        scale = [jnp.exp(each - top) for each in tops]
        total = sum(scale[d] * got_stat[d, 3 * p + 1 : 3 * p + 2, :] for d in range(devices))
        others = sum(scale[d] * got_stat[d, 3 * p + 2 : 3 * p + 3, :] for d in range(devices))
        weights[...] = jnp.zeros_like(weights)
        for d in range(devices):
            weights[d : d + 1, :] = scale[d] / total
        weights[devices : devices + 1, :] = others / total
        weights[...] = jnp.transpose(weights[...])
        parts.append(
            weights[pl.ds(pl.multiple_of((me % per_tile) * block, block), block), :]
        )

    for k in range(1, devices):
        peer = (me + devices - k) % devices
        remote(
            got_msg.at[peer], got_msg.at[peer], msg_send.at[k], msg_recv.at[k], peer
        ).wait_recv()
    results = []
    for p in range(2):
        summed = jnp.zeros((block, LANES), jnp.float32)
        plain = jnp.zeros((block, LANES), jnp.float32)
        for d in range(devices):
            value = got_msg[d, p].astype(jnp.float32)
            summed += value * parts[p][:, d : d + 1]
            plain += value
        results.append((summed, plain, parts[p][:, devices : devices + 1]))
    inside = lax.broadcasted_iota(jnp.int32, (block, LANES), 1) < rank
    (low, low_plain, low_share), (high, high_plain, high_share) = results
    low = low - low_share * pltpu.roll(low_plain, rank, 1)
    high = pltpu.roll(high, rank, 1) - high_share * high_plain
    right[rows_of(me), :] = jnp.where(inside, low, high).astype(jnp.bfloat16)
    for k in range(1, devices):
        start(
            right.at[rows_of(me), :], right.at[rows_of(me), :],
            right_send.at[k], right_recv.at[k], (me + k) % devices,
        )
    for k in range(1, devices):
        peer = (me + devices - k) % devices
        remote(
            right.at[rows_of(peer), :], right.at[rows_of(peer), :],
            right_send.at[k], right_recv.at[k], peer,
        ).wait_recv()

    mine = pl.ds(pl.multiple_of(group * docs, docs), docs)
    height = 8 * docs
    side = lax.broadcasted_iota(jnp.int32, (docs, LANES), 1) < rank
    for n in range(rank // 8):
        rows = pl.ds(n * height, height)
        early = jnp.dot(
            spread[rows, 0:half_rows], right[...], preferred_element_type=jnp.float32
        )
        late = jnp.dot(
            spread[rows, half_rows:tokens], right[...], preferred_element_type=jnp.float32
        )
        for a in range(0, 8, 2):
            even, odd = slice(a * docs, (a + 1) * docs), slice((a + 1) * docs, (a + 2) * docs)
            value = jnp.where(
                side,
                early[even] + pltpu.roll(late[even], rank, 1),
                pltpu.roll(early[odd], rank, 1) + late[odd],
            )
            at = (n * 8 + a) // 2 * LANES
            out_ref[mine, at : at + LANES] = value.astype(jnp.bfloat16)
    for k in range(1, groups):
        start(
            out_ref.at[mine, :], out_ref.at[mine, :],
            group_send.at[k], group_recv.at[k], None, (group + k) % groups,
        )
    for k in range(1, groups):
        other = (group + groups - k) % groups
        theirs = out_ref.at[pl.ds(pl.multiple_of(other * docs, docs), docs), :]
        remote(
            theirs, theirs, group_send.at[k], group_recv.at[k], None, other
        ).wait_recv()
    for k in range(1, devices):
        peer = (me + k) % devices
        remote(
            stat.at[peer // per_tile], got_stat.at[me], stat_send.at[k], stat_recv.at[k], peer
        ).wait_send()
        remote(
            msg.at[:, rows_of(peer), :], got_msg.at[me], msg_send.at[k], msg_recv.at[k], peer
        ).wait_send()
    for copy in sent:
        copy.wait_send()


def document_grads(devices, groups, hidden, weight, proj_in, proj_out, targets, segments):
    tokens, depth = hidden.shape
    width, vocab = weight.shape
    rank = proj_in.shape[1]
    docs = DOC_V * devices
    steps = devices // 4
    block = tokens // (2 * devices)
    vmem = pl.BlockSpec(memory_space=pltpu.VMEM)
    dma = pltpu.SemaphoreType.DMA
    ring = dma((2, steps, 2))
    peers = dma((devices,))
    return pl.pallas_call(
        functools.partial(kernel, devices, groups),
        out_shape=jax.ShapeDtypeStruct((groups * docs, rank * rank), jnp.bfloat16),
        in_specs=[vmem, pl.BlockSpec(memory_space=pl.ANY)] + [vmem] * 4,
        out_specs=vmem,
        scratch_shapes=[
            pltpu.VMEM((devices, tokens, depth), jnp.bfloat16),
            pltpu.VMEM((width, vocab), jnp.bfloat16),
            pltpu.VMEM((tokens, vocab), jnp.float32),
            pltpu.VMEM((tokens, LANES), jnp.float32),
            pltpu.VMEM((LANES, vocab), jnp.bfloat16),
            pltpu.VMEM((LANES, vocab), jnp.bfloat16),
            pltpu.VMEM((LANES, tokens), jnp.float32),
            pltpu.VMEM((docs * rank, tokens), jnp.bfloat16),
            pltpu.VMEM((2, tokens // 2, LANES), jnp.bfloat16),
            pltpu.VMEM((tokens // 2 // LANES, 8, LANES), jnp.float32),
            pltpu.VMEM((devices, 2, block, LANES), jnp.bfloat16),
            pltpu.VMEM((devices, 8, LANES), jnp.float32),
            pltpu.VMEM((LANES, LANES), jnp.float32),
            pltpu.VMEM((tokens // 2, LANES), jnp.bfloat16),
            dma(()), ring, ring, ring, ring, dma((2,)), dma((2,)),
            peers, peers, peers, peers, peers, peers, dma((groups,)), dma((groups,)),
        ],
        compiler_params=pltpu.CompilerParams(
            collective_id=0, has_side_effects=True, vmem_limit_bytes=60 * 1024 * 1024
        ),
    )(
        hidden, weight, proj_in.T, proj_out.T, targets[None, :], segments,
    )


def solution(mesh):
    devices, groups = mesh.shape["vocab"], mesh.shape["tok"]

    def per_device(hidden, weight, proj_in, proj_out, targets, segments, queries):
        grads = document_grads(
            devices, groups, hidden, weight, proj_in, proj_out, targets, segments
        )
        return lax.dot_general(
            grads,
            queries,
            (((1,), (1,)), ((), ())),
            preferred_element_type=jnp.float32,
        )

    return jax.shard_map(
        per_device,
        mesh=mesh,
        in_specs=(
            P("tok", "vocab"),
            P(None, "vocab"),
            P(),
            P("vocab", None),
            P("tok"),
            P("tok", None),
            P(("vocab", "tok"), None),
        ),
        out_specs=P(None, ("vocab", "tok")),
        check_vma=False,
    )
```

time: 89.2 us -> 80.6 us (0.904)
  local copies, waits for them, and re-layouts: 7.39 us -> 0.01 us
  blocking collectives: 6.24 us -> 0 us
  Pallas kernels: 74.3 us -> 78.5 us
  matrix products: 0.89 us -> 1.83 us
    all_gather x1 -> x0, blocking collectives: 6.24 us -> none  [per_device(): lax.all_gather(grads, 'tok', axis=0, tiled=True)]
    pallas_call x1, Pallas kernels: 74.3 us -> 78.5 us  [document_grads(): pl.pallas_call(functools.partial(kernel, devices, groups), out_shape=jax....]
    unnamed x4 -> x2, local copies, waits for them, and re-layouts: 3.49 us -> 0.01 us
    broadcast_in_dim x1 -> x0, local copies, waits for them, and re-layouts: 1.72 us -> none  [document_grads(): targets[:, None]]
    reshape x1 -> x0, local copies, waits for them, and re-layouts: 1.22 us -> none  [per_device(): grads = document_grads(devices, hidden, weight, proj_in, proj_out, target...]
    pad x1 -> x0, local copies, waits for them, and re-layouts: 0.95 us -> none  [document_grads(): jnp.pad(proj_out, ((0, 0), (gap, 0)))]
    dot_general x1, matrix products: 0.89 us -> 1.83 us  [per_device(): lax.dot_general(grads, queries, (((1,), (1,)), ((), ())), preferred_eleme...]
where the time goes in v2:
time: 80.6 us; the launch traced here: 80.4 us
  Pallas kernels  78.5 us (97%)
  matrix products  1.83 us (2%)
    pallas_call x1, Pallas kernels, document_grads(): pl.pallas_call(functools.partial(kernel, devices, groups), out_shape=jax....  78.5 us
    dot_general x1, matrix products, per_device(): lax.dot_general(grads, queries, (((1,), (1,)), ((), ())), preferred_eleme...  1.83 us

profile of v2, /device:TPU:0, one launch (start us, length us, event | category | flops | bytes accessed | tf_op | source)
XLA Modules:
  0.0 80.4 jit_solution(16827783383900479003)
XLA Ops:
  0.0 0.0 copy-start
  0.0 78.5 %shard_map.73 = bf16[32,4096]{1,0:T(8,128)(2,1)} custom-call(bf16[1024,256]{1,0:T(8,128)(2,1)} %h_ref.1, bf16[4096,1024]{1,0:T(8,128)(2,1)} %w_hbm.1, bf16[64,4096]{1,0:T(8,128)(2,1)} %bitcast.5, bf16[64,1024]{1,0:T(8,128)(2,1)} %bitcast.6, s32[1,1024]{1,0:T(1,128)} %bitcast.7, s32[1,1024]{1,0:T(1,128)} %seg_ref.1), custom_call_target="tpu_custom_call" | custom-call | tf_op jit(solution)/shard_map/pallas_call | solution.py:369
  78.6 0.0 copy-done
  78.6 1.8 %fusion = f32[32,64]{1,0:T(8,128)} fusion(bf16[32,4096]{1,0:T(8,128)(2,1)} %shard_map.73, bf16[64,4096]{1,0:T(8,128)(2,1)S(1)} %copy-done), kind=kOutput, calls=%fused_computation | convolution fusion | flops 16777216 | bytes 794624 | tf_op jit(solution)/shard_map/dot_general | solution.py:407
Async XLA Ops:
  0.0 78.6 %copy-start = (bf16[64,4096]{1,0:T(8,128)(2,1)S(1)}, bf16[64,4096]{1,0:T(8,128)(2,1)}, u32[]{:S(2)}) copy-start(bf16[64,4096]{1,0:T(8,128)(2,1)} %param.13) | copy-start | bytes 1572868
